TPU v7x, 128 devices: a whole 4x4x4 slice. The times are simulated.
128 devices in a mesh: batch: 32 (over z, x, core), cols: 4 (over y).
Axes of the slice: x: 4, y: 4, z: 4, core: 2. Of those that a mesh axis runs over, the one named last changes fastest.
Arguments:
- partial_query: float32 [32, 1024, 1024], P('batch', None, 'cols'), may hold values from -1.25 to 1.25
- partial_key: float32 [32, 1024, 1024], P('batch', None, 'cols'), may hold values from -1.25 to 1.25
- partial_value: float32 [32, 1024, 1024], P('batch', None, 'cols'), may hold values from -1.25 to 1.25
- partial_mixed: float32 [32, 1024, 1024], P('batch', 'cols'), may hold values from -1.25 to 1.25
- partial_norm: float32 [32, 1024], P('batch'), may hold values from -12 to 12
- partial_bias: float32 [32, 1024], P('batch'), may hold values from -12 to 12
- master_query: float32 [1024, 1024], P('batch', 'cols'), may hold values from -0.1875 to 0.1875
- master_key: float32 [1024, 1024], P('batch', 'cols'), may hold values from -0.1875 to 0.1875
- master_value: float32 [1024, 1024], P('batch', 'cols'), may hold values from -0.1875 to 0.1875
- master_mixed: float32 [1024, 1024], P('cols', 'batch'), may hold values from -0.1875 to 0.1875
- master_norm: float32 [1024], P('batch'), may hold values from 0.25 to 1.75
- master_bias: float32 [1024], P('batch'), may hold values from -3 to 3
Outputs:
- compute_query: bfloat16 [1024, 1024], P(None, 'cols')
- compute_key: bfloat16 [1024, 1024], P(None, 'cols')
- compute_value: bfloat16 [1024, 1024], P(None, 'cols')
- compute_mixed: bfloat16 [1024, 1024], P('cols')
- compute_norm: bfloat16 [1024], replicated
- compute_bias: bfloat16 [1024], replicated
- stepped_query: float32 [1024, 1024], P('batch', 'cols')
- stepped_key: float32 [1024, 1024], P('batch', 'cols')
- stepped_value: float32 [1024, 1024], P('batch', 'cols')
- stepped_mixed: float32 [1024, 1024], P('cols', 'batch')
- stepped_norm: float32 [1024], P('batch')
- stepped_bias: float32 [1024], P('batch')
All inputs are finite; a program needn't handle non-finite values.
Results may differ from a plain program's by a relative error of at most 0.001.
Values may be sent and summed in bfloat16 or wider, within the bound.
A program may use at most 64 MiB of HBM per device.

v0:
```python
import jax
import jax.numpy as jnp
from jax import lax
from jax.sharding import Mesh
from jax.sharding import PartitionSpec as P

BATCH = ("batch_0", "batch_1", "batch_2")
learn_rate = 0.4


def in_blocks(x, dim, count):
    shape = x.shape
    tiles = x.reshape(*shape[:dim], count, shape[dim] // count, *shape[dim + 1 :])
    return jnp.moveaxis(tiles, dim, 0)


def sent_and_summed(x, axis, dim):
    count = lax.axis_size(axis)
    tiles = lax.all_to_all(in_blocks(x, dim, count), axis, 0, 0, tiled=True)
    return jnp.sum(tiles, axis=0)


def sum_by_axis(x, axes, dim):
    far, near = axes
    own = sent_and_summed(in_blocks(x, dim, lax.axis_size(far)), near, dim + 1)
    return jnp.sum(lax.all_to_all(own, far, 0, 0, tiled=True), axis=0)


def side_by_side(arrays, axis, dim, along):
    ends, at = ([], 0)
    for a in arrays[:-1]:
        at += a.shape[along]
        ends.append(at)
    both = jnp.concatenate(arrays, axis=along)
    return tuple(jnp.split(sum_by_axis(both, axis, dim), ends, axis=along))


def gather_turned(arrays, axis, dims):
    turned = [jnp.moveaxis(a, dim, 0) for a, dim in zip(arrays, dims)]
    both = jnp.concatenate([t.reshape(len(t), -1) for t in turned], axis=1)
    whole, at, done = (lax.all_gather(both, axis, axis=0, tiled=True), 0, [])
    for t, dim in zip(turned, dims):
        share = whole[:, at : at + t[0].size].reshape(-1, *t.shape[1:])
        done.append(jnp.moveaxis(share, 0, dim))
        at += t[0].size
    return tuple(done)


def per_device(
    partial_query,
    partial_key,
    partial_value,
    partial_mixed,
    partial_norm,
    partial_bias,
    master_query,
    master_key,
    master_value,
    master_mixed,
    master_norm,
    master_bias,
):
    mean_query, mean_key, mean_value, mean_mixed, mean_norm, mean_bias = (
        *side_by_side(
            (partial_query[0], partial_key[0], partial_value[0]),
            (("batch_0", "batch_1"), "batch_2"),
            0,
            1,
        ),
        sum_by_axis(partial_mixed[0], (("batch_0", "batch_1"), "batch_2"), 1),
        sum_by_axis(partial_norm[0], (("batch_0", "batch_1"), "batch_2"), 0),
        sum_by_axis(partial_bias[0], (("batch_0", "batch_1"), "batch_2"), 0),
    )
    mean_rate = lax.axis_size(BATCH) ** (-0.5)
    mean_query = mean_query * mean_rate
    mean_key = mean_key * mean_rate
    mean_value = mean_value * mean_rate
    mean_mixed = mean_mixed * mean_rate
    mean_norm = mean_norm * mean_rate
    mean_bias = mean_bias * mean_rate
    stepped_query = master_query - learn_rate * mean_query
    stepped_key = master_key - learn_rate * mean_key
    stepped_value = master_value - learn_rate * mean_value
    stepped_mixed = master_mixed - learn_rate * mean_mixed
    stepped_norm = master_norm - learn_rate * mean_norm
    stepped_bias = master_bias - learn_rate * mean_bias
    compute_query, compute_key, compute_value, compute_mixed, compute_norm, compute_bias = (
        gather_turned(
            (
                stepped_query.astype(jnp.bfloat16),
                stepped_key.astype(jnp.bfloat16),
                stepped_value.astype(jnp.bfloat16),
                stepped_mixed.astype(jnp.bfloat16),
                stepped_norm.astype(jnp.bfloat16),
                stepped_bias.astype(jnp.bfloat16),
            ),
            BATCH,
            (0, 0, 0, 1, 0, 0),
        )
    )
    return (
        compute_query,
        compute_key,
        compute_value,
        compute_mixed,
        compute_norm,
        compute_bias,
        stepped_query,
        stepped_key,
        stepped_value,
        stepped_mixed,
        stepped_norm,
        stepped_bias,
    )


def solution(mesh):
    split = Mesh(
        mesh.devices.reshape(4, 4, 2, mesh.shape["cols"]), ("batch_0", "batch_1", "batch_2", "cols")
    )
    in_specs = (
        P(BATCH, None, "cols"),
        P(BATCH, None, "cols"),
        P(BATCH, None, "cols"),
        P(BATCH, "cols", None),
        P(BATCH, None),
        P(BATCH, None),
        P(BATCH, "cols"),
        P(BATCH, "cols"),
        P(BATCH, "cols"),
        P("cols", BATCH),
        P(BATCH),
        P(BATCH),
    )
    out_specs = (
        P(None, "cols"),
        P(None, "cols"),
        P(None, "cols"),
        P("cols", None),
        P(),
        P(),
        P(BATCH, "cols"),
        P(BATCH, "cols"),
        P(BATCH, "cols"),
        P("cols", BATCH),
        P(BATCH),
        P(BATCH),
    )
    return jax.shard_map(
        per_device, mesh=split, in_specs=in_specs, out_specs=out_specs, check_vma=False
    )
```

profile of v0, /device:TPU:1, one launch (start us, length us, event | category | flops | bytes accessed | tf_op | source)
XLA Modules:
  0.0 161.0 jit_solution(4723989277255362857)
XLA Ops:
  7.7 1.3 reduce.12
  9.8 4.6 %all-to-all-start.4 = ((f32[2,1,512]{2,1,0:T(1,128)}), f32[2,1,512]{2,1,0:T(1,128)S(1)}, u32[]{:S(2)}, u32[]{:S(2)}) async-start(f32[2,1,512]{2,1,0:T(1,128)} %reshape.72), calls=%async_computation.4 | async-start | bytes 8192 | tf_op jit(solution)/shard_map/all_to_all | solution.py:19
  14.4 2.2 %maximum_bitcast_fusion = f32[2,16,32,768]{3,2,0,1:T(8,128)S(1)} fusion(f32[16,2,32,256]{3,2,1,0:T(8,128)} %bitcast.25, f32[16,2,32,256]{3,2,1,0:T(8,128)} %bitcast.26, f32[16,2,32,256]{3,2,1,0:T(8,128)} %bitcast.27), kind=kLoop, calls=%fused_computation | loop fusion | flops 1572864 | bytes 6291456 | tf_op jit(solution)/shard_map/transpose | solution.py:14
  16.6 2.0 %copy.46 = f32[2,16,32,768]{3,2,1,0:T(8,128)} copy(f32[2,16,32,768]{3,2,0,1:T(8,128)S(1)} %maximum_bitcast_fusion) | data formatting | bytes 6291456 | tf_op jit(solution)/shard_map/transpose | solution.py:14
  18.6 4.1 %all-to-all-start = ((f32[2,16,32,768]{3,2,1,0:T(8,128)}), f32[2,16,32,768]{3,2,1,0:T(8,128)S(1)}, u32[]{:S(2)}, u32[]{:S(2)}) async-start(f32[2,16,32,768]{3,2,1,0:T(8,128)} %copy.46), calls=%async_computation | async-start | bytes 6291456 | tf_op jit(solution)/shard_map/all_to_all | solution.py:19
  24.8 2.5 %copy.47 = f32[1,256,1024]{1,2,0:T(8,128)} copy(f32[1,256,1024]{2,1,0:T(8,128)} %param.15) | data formatting | bytes 2097152 | tf_op args[3]
  27.3 2.3 %copy.48 = f32[2,16,256,32]{2,3,1,0:T(8,128)} copy(f32[2,16,256,32]{2,3,0,1:T(8,128)} %bitcast.24) | data formatting | bytes 2097152 | tf_op jit(solution)/shard_map/transpose | solution.py:14
  30.3 3.4 %all_to_all.48 = f32[2,1,512]{2,1,0:T(1,128)S(1)} all-to-all(f32[2,1,512]{2,1,0:T(1,128)S(1)} %reshape.74), channel_id=1, replica_groups=mesh['batch_0'=4,'batch_1'=4,'batch_2'=2,'cols'=4] {'batch_2'}, dimensions={0} | all-to-all | bytes 8192 | tf_op jit(solution)/shard_map/all_to_all | solution.py:19
  33.6 6.5 %all_to_all.49 = f32[2,16,256,32]{2,3,1,0:T(8,128)} all-to-all(f32[2,16,256,32]{2,3,1,0:T(8,128)} %copy.48), channel_id=1, replica_groups=mesh['batch_0'=4,'batch_1'=4,'batch_2'=2,'cols'=4] {'batch_2'}, dimensions={0} | all-to-all | bytes 2097152 | tf_op jit(solution)/shard_map/all_to_all | solution.py:19
  40.2 7.7 %all-to-all-start.5 = ((f32[16,1,32]{2,1,0:T(1,128)}), f32[16,1,32]{2,1,0:T(1,128)S(1)}, u32[]{:S(2)}, u32[]{:S(2)}) async-start(f32[16,1,32]{2,1,0:T(1,128)} %bitcast.10), calls=%async_computation.5 | async-start | bytes 16384 | tf_op jit(solution)/shard_map/all_to_all | solution.py:26
  49.3 5.0 %all-to-all-done.5 = f32[16,1,32]{2,1,0:T(1,128)S(1)} async-done(((f32[16,1,32]{2,1,0:T(1,128)}), f32[16,1,32]{2,1,0:T(1,128)S(1)}, u32[]{:S(2)}, u32[]{:S(2)}) %all-to-all-start.5) | async-done | bytes 2080 | tf_op jit(solution)/shard_map/all_to_all | solution.py:26
  54.3 3.5 %all-to-all-start.7 = ((f32[16,1,32]{2,1,0:T(1,128)}), f32[16,1,32]{2,1,0:T(1,128)S(1)}, u32[]{:S(2)}, u32[]{:S(2)}) async-start(f32[16,1,32]{2,1,0:T(1,128)} %bitcast.13), calls=%async_computation.7 | async-start | bytes 16384 | tf_op jit(solution)/shard_map/all_to_all | solution.py:26
  57.7 2.1 %reduce_sum.74 = f32[16,256,32]{1,2,0:T(8,128)} reduce(f32[2,16,256,32]{2,3,1,0:T(8,128)} %all_to_all.49, f32[]{:T(128)} %constant.6.clone.1), dimensions={0}, to_apply=%region_2.0 | reduce | flops 131072 | bytes 1572868 | tf_op jit(solution)/shard_map/reduce_sum | solution.py:20
  59.9 4.2 %all-to-all-done.7 = f32[16,1,32]{2,1,0:T(1,128)S(1)} async-done(((f32[16,1,32]{2,1,0:T(1,128)}), f32[16,1,32]{2,1,0:T(1,128)S(1)}, u32[]{:S(2)}, u32[]{:S(2)}) %all-to-all-start.7) | async-done | bytes 2080 | tf_op jit(solution)/shard_map/all_to_all | solution.py:26
  64.0 4.2 %all-to-all-start.3 = ((f32[16,256,32]{1,2,0:T(8,128)}), f32[16,256,32]{1,2,0:T(8,128)}, u32[]{:S(2)}, u32[]{:S(2)}) async-start(f32[16,256,32]{1,2,0:T(8,128)} %reduce_sum.74), calls=%async_computation.3 | async-start | bytes 1048576 | tf_op jit(solution)/shard_map/all_to_all | solution.py:26
  68.3 1.5 reduce_sum.72
  69.8 7.4 %all-to-all-done.3 = f32[16,256,32]{1,2,0:T(8,128)} async-done(((f32[16,256,32]{1,2,0:T(8,128)}), f32[16,256,32]{1,2,0:T(8,128)}, u32[]{:S(2)}, u32[]{:S(2)}) %all-to-all-start.3) | async-done | bytes 524320 | tf_op jit(solution)/shard_map/all_to_all | solution.py:26
  77.3 3.7 %all-to-all-start.1 = ((f32[16,32,768]{2,1,0:T(8,128)}), f32[16,32,768]{2,1,0:T(8,128)S(1)}, u32[]{:S(2)}, u32[]{:S(2)}) async-start(f32[16,32,768]{2,1,0:T(8,128)} %reduce_sum.72), calls=%async_computation.1 | async-start | bytes 3145728 | tf_op jit(solution)/shard_map/all_to_all | solution.py:26
  82.3 1.1 reduce_sum.75
  84.1 16.0 %all-to-all-done.1 = f32[16,32,768]{2,1,0:T(8,128)S(1)} async-done(((f32[16,32,768]{2,1,0:T(8,128)}), f32[16,32,768]{2,1,0:T(8,128)S(1)}, u32[]{:S(2)}, u32[]{:S(2)}) %all-to-all-start.1) | async-done | bytes 1572896 | tf_op jit(solution)/shard_map/all_to_all | solution.py:26
  101.6 46.9 %all-gather.2.cloned.1.call-done = bf16[1024,1026]{1,0:T(8,128)(2,1)} async-done(((bf16[32,1026]{1,0:T(8,128)(2,1)}), bf16[1024,1026]{1,0:T(8,128)(2,1)}) %all-gather.2.cloned.1.call-update) | async-done | bytes 2101264 | tf_op jit(solution)/shard_map/all_gather | solution.py:41
  148.5 2.7 %slice_bitcast_fusion = (bf16[256,1024]{0,1:T(8,128)(2,1)S(1)}, bf16[1024,256]{1,0:T(8,128)(2,1)}, bf16[1024,256]{1,0:T(8,128)(2,1)}, bf16[1024,256]{1,0:T(8,128)(2,1)}) fusion(bf16[1024,1026]{1,0:T(8,128)(2,1)} %all-gather.2.cloned.1.call-done), kind=kLoop, calls=%fused_computation.1 | loop fusion | bytes 4194304 | tf_op jit(solution)/shard_map/transpose | solution.py:44
  151.2 1.0 copy.54
  152.2 1.9 %slice_reduce_fusion = (bf16[1024]{0:T(1024)(128)(2,1)}, bf16[1024]{0:T(1024)(128)(2,1)}) fusion(bf16[1024,1026]{1,0:T(8,128)(2,1)} %all-gather.2.cloned.1.call-done), kind=kLoop, calls=%fused_computation.2 | loop fusion | bytes 8192 | tf_op jit(solution)/shard_map/slice | solution.py:43
  (43 shorter events, 8.8 us)
Async XLA Ops:
  9.8 8.8 %all-to-all-start.4 = ((f32[2,1,512]{2,1,0:T(1,128)}), f32[2,1,512]{2,1,0:T(1,128)S(1)}, u32[]{:S(2)}, u32[]{:S(2)}) async-start(f32[2,1,512]{2,1,0:T(1,128)} %reshape.72), calls=%async_computation.4 | async-start | bytes 8192 | tf_op jit(solution)/shard_map/all_to_all | solution.py:19
  18.6 5.4 %copy-start.4 = (f32[1,1024]{1,0:T(1,128)S(1)}, f32[1,1024]{1,0:T(1,128)}, u32[]{:S(2)}) copy-start(f32[1,1024]{1,0:T(1,128)} %param.17) | copy-start | bytes 12292
  18.6 11.7 %all-to-all-start = ((f32[2,16,32,768]{3,2,1,0:T(8,128)}), f32[2,16,32,768]{3,2,1,0:T(8,128)S(1)}, u32[]{:S(2)}, u32[]{:S(2)}) async-start(f32[2,16,32,768]{3,2,1,0:T(8,128)} %copy.46), calls=%async_computation | async-start | bytes 6291456 | tf_op jit(solution)/shard_map/all_to_all | solution.py:19
  40.2 14.1 %all-to-all-start.5 = ((f32[16,1,32]{2,1,0:T(1,128)}), f32[16,1,32]{2,1,0:T(1,128)S(1)}, u32[]{:S(2)}, u32[]{:S(2)}) async-start(f32[16,1,32]{2,1,0:T(1,128)} %bitcast.10), calls=%async_computation.5 | async-start | bytes 16384 | tf_op jit(solution)/shard_map/all_to_all | solution.py:26
  54.3 9.8 %all-to-all-start.7 = ((f32[16,1,32]{2,1,0:T(1,128)}), f32[16,1,32]{2,1,0:T(1,128)S(1)}, u32[]{:S(2)}, u32[]{:S(2)}) async-start(f32[16,1,32]{2,1,0:T(1,128)} %bitcast.13), calls=%async_computation.7 | async-start | bytes 16384 | tf_op jit(solution)/shard_map/all_to_all | solution.py:26
  64.0 13.2 %all-to-all-start.3 = ((f32[16,256,32]{1,2,0:T(8,128)}), f32[16,256,32]{1,2,0:T(8,128)}, u32[]{:S(2)}, u32[]{:S(2)}) async-start(f32[16,256,32]{1,2,0:T(8,128)} %reduce_sum.74), calls=%async_computation.3 | async-start | bytes 1048576 | tf_op jit(solution)/shard_map/all_to_all | solution.py:26
  68.3 12.8 %copy-start.5 = (f32[32]{0:T(128)S(1)}, f32[32]{0:T(128)}, u32[]{:S(2)}) copy-start(f32[32]{0:T(128)} %param.22) | copy-start | bytes 388
  68.3 13.4 %copy-start.6 = (f32[32]{0:T(128)S(1)}, f32[32]{0:T(128)}, u32[]{:S(2)}) copy-start(f32[32]{0:T(128)} %param.23) | copy-start | bytes 388
  68.3 15.1 %copy-start = (f32[256,32]{0,1:T(8,128)S(1)}, f32[256,32]{0,1:T(8,128)}, u32[]{:S(2)}) copy-start(f32[256,32]{0,1:T(8,128)} %param.21) | copy-start | bytes 98308
  69.8 30.4 %copy-start.1 = (f32[32,256]{1,0:T(8,128)S(1)}, f32[32,256]{1,0:T(8,128)}, u32[]{:S(2)}) copy-start(f32[32,256]{1,0:T(8,128)} %param.20) | copy-start | bytes 98308
  69.8 30.4 %copy-start.2 = (f32[32,256]{1,0:T(8,128)S(1)}, f32[32,256]{1,0:T(8,128)}, u32[]{:S(2)}) copy-start(f32[32,256]{1,0:T(8,128)} %param.19) | copy-start | bytes 98308
  69.8 30.4 %copy-start.3 = (f32[32,256]{1,0:T(8,128)S(1)}, f32[32,256]{1,0:T(8,128)}, u32[]{:S(2)}) copy-start(f32[32,256]{1,0:T(8,128)} %param.18) | copy-start | bytes 98308
  77.3 22.8 %all-to-all-start.1 = ((f32[16,32,768]{2,1,0:T(8,128)}), f32[16,32,768]{2,1,0:T(8,128)S(1)}, u32[]{:S(2)}, u32[]{:S(2)}) async-start(f32[16,32,768]{2,1,0:T(8,128)} %reduce_sum.72), calls=%async_computation.1 | async-start | bytes 3145728 | tf_op jit(solution)/shard_map/all_to_all | solution.py:26
  81.0 67.5 %all-gather.2.cloned.1.call-start = ((), (), s32[]{:S(2)}) async-start(), calls=%async_computation.8 | async-start | bytes 2433024 | tf_op jit(solution)/shard_map/all_gather | solution.py:41
Sparse Core Ops, SparseCore 0:
  101.7 46.7 all-gather.1
where the time goes:
time: 162 us; the launch traced here: 161 us
  waiting for transfers between devices  79.5 us (49%)
  starting transfers between devices  27.8 us (17%)
  local copies, waits for them, and re-layouts  15.6 us (10%)
  between operations  14.2 us (9%)
  other arithmetic  13.9 us (9%)
  blocking collectives  9.91 us (6%)
    all_gather x1, waiting for transfers between devices, gather_turned(): whole, at, done = (lax.all_gather(both, axis, axis=0, tiled=True), 0, [])  46.9 us
    all_to_all x4, waiting for transfers between devices, sum_by_axis(): return jnp.sum(lax.all_to_all(own, far, 0, 0, tiled=True), axis=0)  32.6 us
    all_to_all x4, starting transfers between devices, sum_by_axis(): return jnp.sum(lax.all_to_all(own, far, 0, 0, tiled=True), axis=0)  19.1 us
    all_to_all x2, blocking collectives, sent_and_summed(): tiles = lax.all_to_all(in_blocks(x, dim, count), axis, 0, 0, tiled=True)  9.91 us
    all_to_all x2, starting transfers between devices, sent_and_summed(): tiles = lax.all_to_all(in_blocks(x, dim, count), axis, 0, 0, tiled=True)  8.68 us
    unnamed x21, local copies, waits for them, and re-layouts  5 us
    reduce_sum x4, other arithmetic, sent_and_summed(): return jnp.sum(tiles, axis=0)  4.88 us
    transpose x4, local copies, waits for them, and re-layouts, in_blocks(): return jnp.moveaxis(tiles, dim, 0)  4.34 us
  transfers between devices with their start and end apart: 7, of which 5 were waited for; matrix products, arithmetic and copies ran while one was open for 12% of the time, Pallas kernels for 0%

commit v1 on v0

--- a/solution.py
+++ b/solution.py
@@ -6,6 +6,13 @@
 
 BATCH = ("batch_0", "batch_1", "batch_2")
 learn_rate = 0.4
+
+
+def gather_over(x, name, d):
+    peers = lax.axis_size(name)
+    tiles = jnp.stack([x for _ in range(peers)])
+    tiles = lax.all_to_all(tiles, name, split_axis=0, concat_axis=0)
+    return jnp.concatenate(tiles, axis=d)
 
 
 def in_blocks(x, dim, count):
@@ -38,7 +45,7 @@
 def gather_turned(arrays, axis, dims):
     turned = [jnp.moveaxis(a, dim, 0) for a, dim in zip(arrays, dims)]
     both = jnp.concatenate([t.reshape(len(t), -1) for t in turned], axis=1)
-    whole, at, done = (lax.all_gather(both, axis, axis=0, tiled=True), 0, [])
+    whole, at, done = (gather_over(both, axis, 0), 0, [])
     for t, dim in zip(turned, dims):
         share = whole[:, at : at + t[0].size].reshape(-1, *t.shape[1:])
         done.append(jnp.moveaxis(share, 0, dim))

time: 162 us -> 138 us (0.85)
  waiting for transfers between devices: 79.5 us -> 32.7 us
  blocking collectives: 9.91 us -> 49.8 us
  between operations: 14.2 us -> 0.8 us
  local copies, waits for them, and re-layouts: 15.6 us -> 12.5 us
    all_gather x1 -> x0, waiting for transfers between devices: 46.9 us -> none  [gather_turned(): whole, at, done = (lax.all_gather(both, axis, axis=0, tiled=True), 0, [])]
    all_to_all x0 -> x1, blocking collectives: none -> 39.9 us  [gather_over(): tiles = lax.all_to_all(tiles, name, split_axis=0, concat_axis=0)]
  transfers between devices with their start and end apart: 7 -> 6, of which waited for: 5 -> 4; matrix products, arithmetic and copies ran while one was open for 12% -> 14% of each run, Pallas kernels for 0% -> 0%
where the time goes in v1:
time: 138 us
  blocking collectives  49.8 us (36%)
  waiting for transfers between devices  32.7 us (24%)
  starting transfers between devices  27.8 us (20%)
  other arithmetic  13.9 us (10%)
  local copies, waits for them, and re-layouts  12.5 us (9%)
    all_to_all x1, blocking collectives, gather_over(): tiles = lax.all_to_all(tiles, name, split_axis=0, concat_axis=0)  39.9 us
    all_to_all x4, waiting for transfers between devices, sum_by_axis(): return jnp.sum(lax.all_to_all(own, far, 0, 0, tiled=True), axis=0)  32.7 us
    all_to_all x4, starting transfers between devices, sum_by_axis(): return jnp.sum(lax.all_to_all(own, far, 0, 0, tiled=True), axis=0)  19.1 us
    all_to_all x2, blocking collectives, sent_and_summed(): tiles = lax.all_to_all(in_blocks(x, dim, count), axis, 0, 0, tiled=True)  9.91 us
    all_to_all x2, starting transfers between devices, sent_and_summed(): tiles = lax.all_to_all(in_blocks(x, dim, count), axis, 0, 0, tiled=True)  8.68 us
    unnamed x21, local copies, waits for them, and re-layouts  5 us
    reduce_sum x4, other arithmetic, sent_and_summed(): return jnp.sum(tiles, axis=0)  4.88 us
    transpose x4, local copies, waits for them, and re-layouts, in_blocks(): return jnp.moveaxis(tiles, dim, 0)  4.34 us
  transfers between devices with their start and end apart: 6, of which 4 were waited for; matrix products, arithmetic and copies ran while one was open for 14% of the time, Pallas kernels for 0%

profile of v1, /device:TPU:1, one launch (start us, length us, event | category | flops | bytes accessed | tf_op | source)
XLA Modules:
  0.0 137.6 jit_solution(982677774579907856)
XLA Ops:
  1.2 1.3 reduce.12
  3.3 4.6 %all-to-all-start.4 = ((f32[2,1,512]{2,1,0:T(1,128)}), f32[2,1,512]{2,1,0:T(1,128)S(1)}, u32[]{:S(2)}, u32[]{:S(2)}) async-start(f32[2,1,512]{2,1,0:T(1,128)} %reshape.78), calls=%async_computation.4 | async-start | bytes 8192 | tf_op jit(solution)/shard_map/all_to_all | solution.py:26
  7.9 2.2 %maximum_bitcast_fusion = f32[2,16,32,768]{3,2,0,1:T(8,128)S(1)} fusion(f32[16,2,32,256]{3,2,1,0:T(8,128)} %bitcast.28, f32[16,2,32,256]{3,2,1,0:T(8,128)} %bitcast.29, f32[16,2,32,256]{3,2,1,0:T(8,128)} %bitcast.30), kind=kLoop, calls=%fused_computation | loop fusion | flops 1572864 | bytes 6291456 | tf_op jit(solution)/shard_map/transpose | solution.py:21
  10.1 2.0 %copy.53 = f32[2,16,32,768]{3,2,1,0:T(8,128)} copy(f32[2,16,32,768]{3,2,0,1:T(8,128)S(1)} %maximum_bitcast_fusion) | data formatting | bytes 6291456 | tf_op jit(solution)/shard_map/transpose | solution.py:21
  12.1 4.1 %all-to-all-start = ((f32[2,16,32,768]{3,2,1,0:T(8,128)}), f32[2,16,32,768]{3,2,1,0:T(8,128)S(1)}, u32[]{:S(2)}, u32[]{:S(2)}) async-start(f32[2,16,32,768]{3,2,1,0:T(8,128)} %copy.53), calls=%async_computation | async-start | bytes 6291456 | tf_op jit(solution)/shard_map/all_to_all | solution.py:26
  18.3 2.5 %copy.54 = f32[1,256,1024]{1,2,0:T(8,128)} copy(f32[1,256,1024]{2,1,0:T(8,128)} %param.15) | data formatting | bytes 2097152 | tf_op args[3]
  20.8 2.3 %copy.55 = f32[2,16,256,32]{2,3,1,0:T(8,128)} copy(f32[2,16,256,32]{2,3,0,1:T(8,128)} %bitcast.27) | data formatting | bytes 2097152 | tf_op jit(solution)/shard_map/transpose | solution.py:21
  23.7 3.4 %all_to_all.53 = f32[2,1,512]{2,1,0:T(1,128)S(1)} all-to-all(f32[2,1,512]{2,1,0:T(1,128)S(1)} %reshape.80), channel_id=1, replica_groups=mesh['batch_0'=4,'batch_1'=4,'batch_2'=2,'cols'=4] {'batch_2'}, dimensions={0} | all-to-all | bytes 8192 | tf_op jit(solution)/shard_map/all_to_all | solution.py:26
  27.1 6.5 %all_to_all.54 = f32[2,16,256,32]{2,3,1,0:T(8,128)} all-to-all(f32[2,16,256,32]{2,3,1,0:T(8,128)} %copy.55), channel_id=1, replica_groups=mesh['batch_0'=4,'batch_1'=4,'batch_2'=2,'cols'=4] {'batch_2'}, dimensions={0} | all-to-all | bytes 2097152 | tf_op jit(solution)/shard_map/all_to_all | solution.py:26
  33.6 7.7 %all-to-all-start.5 = ((f32[16,1,32]{2,1,0:T(1,128)}), f32[16,1,32]{2,1,0:T(1,128)S(1)}, u32[]{:S(2)}, u32[]{:S(2)}) async-start(f32[16,1,32]{2,1,0:T(1,128)} %bitcast.10), calls=%async_computation.5 | async-start | bytes 16384 | tf_op jit(solution)/shard_map/all_to_all | solution.py:33
  42.7 5.0 %all-to-all-done.5 = f32[16,1,32]{2,1,0:T(1,128)S(1)} async-done(((f32[16,1,32]{2,1,0:T(1,128)}), f32[16,1,32]{2,1,0:T(1,128)S(1)}, u32[]{:S(2)}, u32[]{:S(2)}) %all-to-all-start.5) | async-done | bytes 2080 | tf_op jit(solution)/shard_map/all_to_all | solution.py:33
  47.7 3.5 %all-to-all-start.7 = ((f32[16,1,32]{2,1,0:T(1,128)}), f32[16,1,32]{2,1,0:T(1,128)S(1)}, u32[]{:S(2)}, u32[]{:S(2)}) async-start(f32[16,1,32]{2,1,0:T(1,128)} %bitcast.13), calls=%async_computation.7 | async-start | bytes 16384 | tf_op jit(solution)/shard_map/all_to_all | solution.py:33
  51.2 2.1 %reduce_sum.74 = f32[16,256,32]{1,2,0:T(8,128)} reduce(f32[2,16,256,32]{2,3,1,0:T(8,128)} %all_to_all.54, f32[]{:T(128)} %constant.6.clone.1), dimensions={0}, to_apply=%region_2.0 | reduce | flops 131072 | bytes 1572868 | tf_op jit(solution)/shard_map/reduce_sum | solution.py:27
  53.3 4.2 %all-to-all-done.7 = f32[16,1,32]{2,1,0:T(1,128)S(1)} async-done(((f32[16,1,32]{2,1,0:T(1,128)}), f32[16,1,32]{2,1,0:T(1,128)S(1)}, u32[]{:S(2)}, u32[]{:S(2)}) %all-to-all-start.7) | async-done | bytes 2080 | tf_op jit(solution)/shard_map/all_to_all | solution.py:33
  57.5 4.2 %all-to-all-start.3 = ((f32[16,256,32]{1,2,0:T(8,128)}), f32[16,256,32]{1,2,0:T(8,128)}, u32[]{:S(2)}, u32[]{:S(2)}) async-start(f32[16,256,32]{1,2,0:T(8,128)} %reduce_sum.74), calls=%async_computation.3 | async-start | bytes 1048576 | tf_op jit(solution)/shard_map/all_to_all | solution.py:33
  61.8 1.5 %reduce_sum.72 = f32[16,32,768]{2,1,0:T(8,128)} reduce(f32[2,16,32,768]{3,2,1,0:T(8,128)S(1)} %all-to-all-done, f32[]{:T(128)} %constant.6.clone.1), dimensions={0}, to_apply=%region_0.0 | reduce | flops 393216 | bytes 4718596 | tf_op jit(solution)/shard_map/reduce_sum | solution.py:27
  63.3 7.4 %all-to-all-done.3 = f32[16,256,32]{1,2,0:T(8,128)} async-done(((f32[16,256,32]{1,2,0:T(8,128)}), f32[16,256,32]{1,2,0:T(8,128)}, u32[]{:S(2)}, u32[]{:S(2)}) %all-to-all-start.3) | async-done | bytes 524320 | tf_op jit(solution)/shard_map/all_to_all | solution.py:33
  70.7 3.7 %all-to-all-start.1 = ((f32[16,32,768]{2,1,0:T(8,128)}), f32[16,32,768]{2,1,0:T(8,128)S(1)}, u32[]{:S(2)}, u32[]{:S(2)}) async-start(f32[16,32,768]{2,1,0:T(8,128)} %reduce_sum.72), calls=%async_computation.1 | async-start | bytes 3145728 | tf_op jit(solution)/shard_map/all_to_all | solution.py:33
  75.8 1.1 reduce_sum.75
  77.5 16.1 %all-to-all-done.1 = f32[16,32,768]{2,1,0:T(8,128)S(1)} async-done(((f32[16,32,768]{2,1,0:T(8,128)}), f32[16,32,768]{2,1,0:T(8,128)S(1)}, u32[]{:S(2)}, u32[]{:S(2)}) %all-to-all-start.1) | async-done | bytes 1572896 | tf_op jit(solution)/shard_map/all_to_all | solution.py:33
  94.6 39.9 %all_to_all.55 = bf16[32,32,1026]{2,1,0:T(8,128)(2,1)S(1)} all-to-all(bf16[32,32,1026]{2,1,0:T(8,128)(2,1)S(1)} %stack.2), channel_id=1, replica_groups=mesh['batch_0'=4,'batch_1'=4,'batch_2'=2,'cols'=4] {'batch_0','batch_1',..., dimensions={0} | all-to-all | bytes 4202496 | tf_op jit(solution)/shard_map/all_to_all | solution.py:14
  134.5 1.2 slice_bitcast_fusion
  135.7 0.9 slice_reduce_fusion
  136.6 1.0 copy.61
  (42 shorter events, 8.3 us)
Async XLA Ops:
  3.3 8.8 %all-to-all-start.4 = ((f32[2,1,512]{2,1,0:T(1,128)}), f32[2,1,512]{2,1,0:T(1,128)S(1)}, u32[]{:S(2)}, u32[]{:S(2)}) async-start(f32[2,1,512]{2,1,0:T(1,128)} %reshape.78), calls=%async_computation.4 | async-start | bytes 8192 | tf_op jit(solution)/shard_map/all_to_all | solution.py:26
  12.1 5.4 %copy-start.4 = (f32[1,1024]{1,0:T(1,128)S(1)}, f32[1,1024]{1,0:T(1,128)}, u32[]{:S(2)}) copy-start(f32[1,1024]{1,0:T(1,128)} %param.17) | copy-start | bytes 12292
  12.1 11.7 %all-to-all-start = ((f32[2,16,32,768]{3,2,1,0:T(8,128)}), f32[2,16,32,768]{3,2,1,0:T(8,128)S(1)}, u32[]{:S(2)}, u32[]{:S(2)}) async-start(f32[2,16,32,768]{3,2,1,0:T(8,128)} %copy.53), calls=%async_computation | async-start | bytes 6291456 | tf_op jit(solution)/shard_map/all_to_all | solution.py:26
  33.6 14.1 %all-to-all-start.5 = ((f32[16,1,32]{2,1,0:T(1,128)}), f32[16,1,32]{2,1,0:T(1,128)S(1)}, u32[]{:S(2)}, u32[]{:S(2)}) async-start(f32[16,1,32]{2,1,0:T(1,128)} %bitcast.10), calls=%async_computation.5 | async-start | bytes 16384 | tf_op jit(solution)/shard_map/all_to_all | solution.py:33
  47.7 9.8 %all-to-all-start.7 = ((f32[16,1,32]{2,1,0:T(1,128)}), f32[16,1,32]{2,1,0:T(1,128)S(1)}, u32[]{:S(2)}, u32[]{:S(2)}) async-start(f32[16,1,32]{2,1,0:T(1,128)} %bitcast.13), calls=%async_computation.7 | async-start | bytes 16384 | tf_op jit(solution)/shard_map/all_to_all | solution.py:33
  57.5 13.2 %all-to-all-start.3 = ((f32[16,256,32]{1,2,0:T(8,128)}), f32[16,256,32]{1,2,0:T(8,128)}, u32[]{:S(2)}, u32[]{:S(2)}) async-start(f32[16,256,32]{1,2,0:T(8,128)} %reduce_sum.74), calls=%async_computation.3 | async-start | bytes 1048576 | tf_op jit(solution)/shard_map/all_to_all | solution.py:33
  61.7 12.8 %copy-start.5 = (f32[32]{0:T(128)S(1)}, f32[32]{0:T(128)}, u32[]{:S(2)}) copy-start(f32[32]{0:T(128)} %param.22) | copy-start | bytes 388
  61.8 13.4 %copy-start.6 = (f32[32]{0:T(128)S(1)}, f32[32]{0:T(128)}, u32[]{:S(2)}) copy-start(f32[32]{0:T(128)} %param.23) | copy-start | bytes 388
  61.8 15.1 %copy-start = (f32[256,32]{0,1:T(8,128)S(1)}, f32[256,32]{0,1:T(8,128)}, u32[]{:S(2)}) copy-start(f32[256,32]{0,1:T(8,128)} %param.21) | copy-start | bytes 98308
  63.3 30.4 %copy-start.1 = (f32[32,256]{1,0:T(8,128)S(1)}, f32[32,256]{1,0:T(8,128)}, u32[]{:S(2)}) copy-start(f32[32,256]{1,0:T(8,128)} %param.20) | copy-start | bytes 98308
  63.3 30.4 %copy-start.2 = (f32[32,256]{1,0:T(8,128)S(1)}, f32[32,256]{1,0:T(8,128)}, u32[]{:S(2)}) copy-start(f32[32,256]{1,0:T(8,128)} %param.19) | copy-start | bytes 98308
  63.3 30.4 %copy-start.3 = (f32[32,256]{1,0:T(8,128)S(1)}, f32[32,256]{1,0:T(8,128)}, u32[]{:S(2)}) copy-start(f32[32,256]{1,0:T(8,128)} %param.18) | copy-start | bytes 98308
  70.7 22.8 %all-to-all-start.1 = ((f32[16,32,768]{2,1,0:T(8,128)}), f32[16,32,768]{2,1,0:T(8,128)S(1)}, u32[]{:S(2)}, u32[]{:S(2)}) async-start(f32[16,32,768]{2,1,0:T(8,128)} %reduce_sum.72), calls=%async_computation.1 | async-start | bytes 3145728 | tf_op jit(solution)/shard_map/all_to_all | solution.py:33
